TPU v7x, 32 devices: a whole 2x2x4 slice. The times are simulated.
32 devices in a mesh: sy: 4 (over y, x), sx: 4 (over z), wl: 2 (over core).
Axes of the slice: x: 2, y: 2, z: 4, core: 2. Of those that a mesh axis runs over, the one named last changes fastest.
Arguments:
- interface_map: bfloat16 [8, 4, 1536, 2, 1536], P(('wl', 'sy'), 'sx'), parts along dimension 0, may hold values from -0.0625 to 0.0625
- source_trace: float32 [8, 4, 2, 64, 4, 384], P(('wl', 'sy'), 'sx'), parts along dimension 0, may hold values from -6 to 6
- restriction: float32 [8, 4, 2, 32, 4, 384], P(('wl', 'sy'), 'sx'), parts along dimension 0, may hold values from -0.02734375 to 0.02734375
- prolongation: float32 [8, 4, 2, 32, 4, 384], P(('wl', 'sy'), 'sx'), parts along dimension 0, may hold values from -0.109375 to 0.109375
- coarse_inverse: float32 [4, 32, 32], P('wl'), parts along dimension 0, may hold values from -0.75 to 0.75
Outputs:
- traces: float32 [8, 4, 2, 64, 4, 384], P(('wl', 'sy'), 'sx'), parts along dimension 0
- coarse_coef: float32 [4, 64, 32], P('wl'), parts along dimension 0
There are 2 independent parts, one for each index of `wl`. A program takes and returns all parts, laid end to end along the dimension named above; each array names one. Nothing has to cross between parts.
All inputs are finite; a program needn't handle non-finite values.
Results may differ from a plain program's by a relative error of at most 0.0025.
Values sent between devices are 32-bit elements; how exact they have to be, the bound alone decides.
A program may use at most 128 MiB of HBM per device.

v0:
```python
import functools

import jax
import jax.numpy as jnp
from jax import lax
from jax.experimental import pallas as pl
from jax.experimental.pallas import tpu as pltpu
from jax.sharding import PartitionSpec as P

ITERS = 6
LANES = 128
F32, BF16 = jnp.float32, jnp.bfloat16
MESH = pl.DeviceIdType.MESH
PRECISE = lax.Precision.HIGHEST
NT = (((1,), (1,)), ((), ()))


def dot(a, b):
    return jnp.dot(a, b, preferred_element_type=F32)


def dot_nt(a, b):
    return lax.dot_general(a, b, NT, preferred_element_type=F32)


def split(x):
    hi = x.astype(BF16)
    return hi, (x - hi.astype(F32)).astype(BF16)


def sweep_kernel(
    ny, nx, iters,
    map_ref, src_ref, rest_ref, lift_ref, inv_ref,
    traces_ref, coef_ref,
    out, recv, wrecv, cbuf, crecv, wcbuf, wcrecv, lhs, ext_lhs, ext_rhs,
    wts, part, xs, rowsum, ys,
    side_send, side_recv, diag_send, diag_recv,
    wside_send, wside_recv, wdiag_send, wdiag_recv,
    x_send, x_recv, y_send, y_recv, inv_full,
):
    rows, k = src_ref.shape
    side = k // 4
    nsrc = rows // 2
    nw_rows = rest_ref.shape[0]
    nc = nw_rows // 2
    half = nsrc // 2
    y, x = lax.axis_index("sy"), lax.axis_index("sx")
    up, dn, lf, rt = y > 0, y < ny - 1, x > 0, x < nx - 1
    sides = ((up, -1, 0), (dn, 1, 0), (lf, 0, -1), (rt, 0, 1))
    diags = (
        (up & lf, -1, -1),
        (up & rt, -1, 1),
        (dn & lf, 1, -1),
        (dn & rt, 1, 1),
    )

    def lanes(s):
        return pl.ds(s * side, side)

    def copies(src, dst, corner_src, corner_dst, ssem, rsem, dsem, drsem):
        flat, diag, flat_in, diag_in = [], [], [], []
        for d, (cond, dy, dx) in enumerate(sides):
            o = d ^ 1
            dev = {"sy": y + dy, "sx": x + dx}
            flat.append((cond, pltpu.make_async_remote_copy(
                src.at[:, lanes(d)], dst.at[:, lanes(o)], ssem.at[d], rsem.at[o],
                device_id=dev, device_id_type=MESH)))
            flat_in.append((cond, pltpu.make_async_remote_copy(
                src.at[:, lanes(d)], dst.at[:, lanes(d)], ssem.at[d], rsem.at[d],
                device_id=dev, device_id_type=MESH)))
        for d, (cond, dy, dx) in enumerate(diags):
            o = 3 - d
            dev = {"sy": y + dy, "sx": x + dx}
            diag.append((cond, pltpu.make_async_remote_copy(
                corner_src, corner_dst.at[o], dsem.at[d], drsem.at[o],
                device_id=dev, device_id_type=MESH)))
            diag_in.append((cond, pltpu.make_async_remote_copy(
                corner_src, corner_dst.at[d], dsem.at[d], drsem.at[d],
                device_id=dev, device_id_type=MESH)))
        return flat, diag, flat_in, diag_in

    def each(items, what):
        for cond, c in items:
            pl.when(cond)(getattr(c, what))

    def pack_corners(ref, dst, scale):
        def column(s, last):
            if last:
                return ref[:, (s + 1) * side - LANES:(s + 1) * side][:, LANES - 1:]
            return ref[:, s * side:s * side + LANES][:, 0:1]

        n = ref.shape[0]
        lane = lax.broadcasted_iota(jnp.int32, (n, LANES), 1)
        block = jnp.zeros((n, LANES), F32)
        for j, (a, b) in enumerate((
            ((0, 0), (2, 0)), ((0, 1), (3, 0)), ((1, 0), (2, 1)), ((1, 1), (3, 1)),
        )):
            block = jnp.where(lane == j, column(*a) + column(*b), block)
        if scale != 1.0:
            block = block * scale
        if n < LANES:
            block = jnp.concatenate([block, jnp.zeros((LANES - n, LANES), F32)], axis=0)
        dst[...] = block.T[:8]

    def assemble(get, get_corner, n, scale, write):
        row = lax.broadcasted_iota(jnp.int32, (LANES, LANES), 0)
        block = jnp.zeros((LANES, LANES), F32)
        for j in range(4):
            block = jnp.where(row == j, get_corner(j)[3 - j:4 - j], block)
        cols = block.T[:n] * scale
        lane = lax.broadcasted_iota(jnp.int32, (n, LANES), 1)
        ends = ((0, 1), (2, 3), (0, 2), (1, 3))
        for s in range(4):
            for t in range(side // LANES):
                at = s * side + t * LANES
                v = get(at)
                if t == 0:
                    j = ends[s][0]
                    v = v + jnp.where(lane == 0, cols[:, j:j + 1], 0.0)
                if t == side // LANES - 1:
                    j = ends[s][1]
                    v = v + jnp.where(lane == LANES - 1, cols[:, j:j + 1], 0.0)
                write(at, v)

    for d, (cond, _, _) in enumerate(sides):
        @pl.when(jnp.logical_not(cond))
        def _(d=d):
            for slot in range(2):
                recv[slot, :, lanes(d)] = jnp.zeros((rows, side), F32)
            wrecv[:, lanes(d)] = jnp.zeros((nw_rows, side), F32)
    for d, (cond, _, _) in enumerate(diags):
        @pl.when(jnp.logical_not(cond))
        def _(d=d):
            for slot in range(2):
                crecv[slot, d] = jnp.zeros((8, LANES), F32)
            wcrecv[d] = jnp.zeros((8, LANES), F32)

    w_flat, w_diag, w_flat_in, w_diag_in = copies(
        rest_ref, wrecv, wcbuf, wcrecv, wside_send, wside_recv, wdiag_send, wdiag_recv)
    pack_corners(rest_ref, wcbuf, 0.5)
    each(w_diag, "start")
    each(w_flat, "start")

    def exchange(slot, src):
        return copies(
            src, recv.at[slot], cbuf.at[slot], crecv.at[slot],
            side_send.at[slot], side_recv.at[slot], diag_send.at[slot], diag_recv.at[slot])

    def x_copies(slot):
        res = []
        for d in range(1, nx):
            peer = lax.rem(x + d, nx)
            res.append((
                pltpu.make_async_remote_copy(
                    part.at[slot], xs.at[slot, x], x_send.at[slot, d], x_recv.at[slot, d],
                    device_id={"sy": y, "sx": peer}, device_id_type=MESH),
                pltpu.make_async_remote_copy(
                    part.at[slot], xs.at[slot, lax.rem(x + nx - d, nx)],
                    x_send.at[slot, d], x_recv.at[slot, d],
                    device_id={"sy": y, "sx": peer}, device_id_type=MESH)))
        return res

    def y_copies(slot):
        res = []
        for d in range(1, ny):
            peer = lax.rem(y + d, ny)
            res.append((
                pltpu.make_async_remote_copy(
                    rowsum.at[slot], ys.at[slot, y], y_send.at[slot, d], y_recv.at[slot, d],
                    device_id={"sy": peer, "sx": x}, device_id_type=MESH),
                pltpu.make_async_remote_copy(
                    rowsum.at[slot], ys.at[slot, lax.rem(y + ny - d, ny)],
                    y_send.at[slot, d], y_recv.at[slot, d],
                    device_id={"sy": peer, "sx": x}, device_id_type=MESH)))
        return res

    def restrict_start(slot, src):
        re_hi, re_lo = split(src[:nsrc])
        im_hi, im_lo = split(src[nsrc:])
        a_hi, a_lo, b_hi, b_lo = (wts[i] for i in range(4))
        t = dot_nt(re_hi, a_hi) + dot_nt(im_hi, b_hi)
        t = t + (dot_nt(re_lo, a_hi) + dot_nt(im_lo, b_hi))
        t = t + (dot_nt(re_hi, a_lo) + dot_nt(im_hi, b_lo))
        lane = lax.broadcasted_iota(jnp.int32, (half, LANES), 1)
        t = jnp.where(lane < 2 * nc, t[:half], t[half:])
        part[slot] = t
        xs[slot, x] = t
        for c, _ in x_copies(slot):
            c.start()

    def restrict_turn(slot):
        for _, c in x_copies(slot):
            c.wait_recv()
        t = xs[slot, 0]
        for i in range(1, nx):
            t = t + xs[slot, i]
        rowsum[slot] = t
        ys[slot, y] = t
        for c, _ in y_copies(slot):
            c.start()

    def coarse(slot):
        for _, c in y_copies(slot):
            c.wait_recv()
        t = ys[slot, 0]
        for i in range(1, ny):
            t = t + ys[slot, i]
        lane = lax.broadcasted_iota(jnp.int32, (half, LANES), 1)
        low = lane < 2 * nc
        t = jnp.concatenate([jnp.where(low, t, 0.0), jnp.where(low, 0.0, t)], axis=0)
        c_re = jnp.dot(t, inv_full[0], preferred_element_type=F32, precision=PRECISE)
        c_im = jnp.dot(t, inv_full[1], preferred_element_type=F32, precision=PRECISE)
        c = jnp.concatenate([c_re, c_im], axis=0)
        coef_ref[0] = c_re[:, :nc]
        coef_ref[1] = c_im[:, :nc]
        hi, lo = split(c)
        lane = lax.broadcasted_iota(jnp.int32, (rows, LANES), 1)
        mid = (lane >= nc) & (lane < 2 * nc)
        ext_lhs[...] = jnp.where(mid, lo.astype(F32), hi.astype(F32)).astype(BF16)

    def restrict_end(slot):
        for c, _ in x_copies(slot):
            c.wait_send()
        for c, _ in y_copies(slot):
            c.wait_send()

    flat, diag, flat_in, diag_in = exchange(0, src_ref)
    pack_corners(src_ref, cbuf.at[0], 1.0)
    each(diag, "start")
    each(flat, "start")

    cr, ci = inv_ref[0], inv_ref[1]
    blank = jnp.zeros((nc, LANES - 3 * nc), F32)
    for i, (top, bottom) in enumerate(((cr, -ci), (ci, cr))):
        for j, v in enumerate((top, bottom, top, bottom)):
            inv_full[i, j * nc:(j + 1) * nc] = jnp.concatenate([v, v, v, blank], axis=1)

    lift_hi, lift_lo = split(lift_ref[...])
    lhs[...] = jnp.concatenate([lift_hi, lift_lo], axis=0)
    for s in range(4):
        p = dot(lhs[...], map_ref[:, s * side:(s + 1) * side])
        q = dot(lhs[...], map_ref[:, k + s * side:k + (s + 1) * side])
        p = p[:nw_rows] + p[nw_rows:]
        q = q[:nw_rows] + q[nw_rows:]
        for at, v in ((s * side, p[:nc] - q[nc:]), (k + s * side, q[:nc] + p[nc:])):
            hi, lo = split(v)
            ext_rhs[:, at:at + side] = jnp.concatenate(
                [hi, hi, lo, jnp.zeros((LANES - 3 * nc, side), BF16)], axis=0)

    each(w_flat_in, "wait_recv")
    each(w_diag_in, "wait_recv")

    def write_weights(at, v):
        wr, wi = v[:nc], v[nc:]
        for i, rowset in ((0, [wr, wi, wr, wi]), (2, [-wi, wr, -wi, wr])):
            hi, lo = split(jnp.concatenate(rowset, axis=0))
            wts[i, :, at:at + LANES] = hi
            wts[i + 1, :, at:at + LANES] = lo

    assemble(lambda at: wrecv[:, at:at + LANES], lambda j: wcrecv[j], nw_rows, 1.0, write_weights)
    restrict_start(0, src_ref)
    restrict_turn(0)
    each(w_flat, "wait_send")
    each(w_diag, "wait_send")

    def store_lhs(at, v):
        lhs[:, at:at + LANES] = v.astype(BF16)

    def step(it, carry):
        old = lax.rem(it + 1, 2)
        new = lax.rem(it, 2)
        flat, diag, flat_in, diag_in = exchange(old, out)
        each(diag_in, "wait_recv")
        each(flat_in, "wait_recv")
        assemble(lambda at: recv[old, :, at:at + LANES], lambda j: crecv[old, j], rows, 0.5, store_lhs)
        each(flat, "wait_send")
        each(diag, "wait_send")
        for s in range(4):
            at = s * side
            p = dot(lhs[...], map_ref[:, at:at + side])
            q = dot(lhs[...], map_ref[:, k + at:k + at + side])
            out[:nsrc, at:at + side] = p[:nsrc] - q[nsrc:] + src_ref[:nsrc, at:at + side]
            out[nsrc:, at:at + side] = q[:nsrc] + p[nsrc:] + src_ref[nsrc:, at:at + side]
        coarse(old)
        restrict_end(old)
        for s in range(4):
            at = s * side
            p = dot(ext_lhs[...], ext_rhs[:, at:at + side])
            q = dot(ext_lhs[...], ext_rhs[:, k + at:k + at + side])
            out[:nsrc, at:at + side] += p[:nsrc] - q[nsrc:]
            out[nsrc:, at:at + side] += q[:nsrc] + p[nsrc:]
        flat, diag, _, _ = exchange(new, out)
        pack_corners(out, cbuf.at[new], 1.0)
        each(diag, "start")

        each(flat, "start")

        @pl.when(it < iters - 1)
        def _():
            restrict_start(new, out)
            restrict_turn(new)

        return carry

    lax.fori_loop(1, iters, step, 0)

    last = (iters - 1) % 2
    flat, diag, flat_in, diag_in = exchange(last, out)
    each(diag_in, "wait_recv")
    each(flat_in, "wait_recv")

    def store_out(at, v):
        traces_ref[:, at:at + LANES] = v

    assemble(lambda at: recv[last, :, at:at + LANES], lambda j: crecv[last, j], rows, 0.5, store_out)
    each(flat, "wait_send")
    each(diag, "wait_send")


def per_device(ny, nx, interface_map, source_trace, restriction, prolongation, coarse_inverse):
    _, _, _, nsrc, _, side = source_trace.shape
    nc = restriction.shape[3]
    k, rows = 4 * side, 2 * nsrc
    table = interface_map.reshape(k, 2 * k)
    src = source_trace.reshape(rows, k)
    rest = restriction.reshape(2 * nc, k)
    lift = prolongation.reshape(2 * nc, k)
    half = nsrc // 2
    dma = pltpu.SemaphoreType.DMA
    vmem = pl.BlockSpec(memory_space=pltpu.VMEM)
    traces, coef = pl.pallas_call(
        functools.partial(sweep_kernel, ny, nx, ITERS),
        out_shape=(
            jax.ShapeDtypeStruct((rows, k), F32),
            jax.ShapeDtypeStruct((2, nsrc, nc), F32),
        ),
        in_specs=[vmem] * 5,
        out_specs=(vmem, vmem),
        scratch_shapes=[
            pltpu.VMEM((rows, k), F32),
            pltpu.VMEM((2, rows, k), F32),
            pltpu.VMEM((2 * nc, k), F32),
            pltpu.VMEM((2, 8, LANES), F32),
            pltpu.VMEM((2, 4, 8, LANES), F32),
            pltpu.VMEM((8, LANES), F32),
            pltpu.VMEM((4, 8, LANES), F32),
            pltpu.VMEM((rows, k), BF16),
            pltpu.VMEM((rows, LANES), BF16),
            pltpu.VMEM((LANES, 2 * k), BF16),
            pltpu.VMEM((4, 4 * nc, k), BF16),
            pltpu.VMEM((2, half, LANES), F32),
            pltpu.VMEM((2, nx, half, LANES), F32),
            pltpu.VMEM((2, half, LANES), F32),
            pltpu.VMEM((2, ny, half, LANES), F32),
            dma((2, 4)), dma((2, 4)), dma((2, 4)), dma((2, 4)),
            dma((4,)), dma((4,)), dma((4,)), dma((4,)),
            dma((2, nx)), dma((2, nx)), dma((2, ny)), dma((2, ny)),
            pltpu.VMEM((2, 4 * nc, LANES), F32),
        ],
        compiler_params=pltpu.CompilerParams(
            has_side_effects=True, vmem_limit_bytes=48 * 1024 * 1024
        ),
    )(table, src, rest, lift, coarse_inverse)
    return (
        traces.reshape(source_trace.shape),
        coef,
    )


def solution(mesh):
    return jax.shard_map(
        functools.partial(per_device, mesh.shape["sy"], mesh.shape["sx"]),
        mesh=mesh,
        in_specs=(
            P(("wl", "sy"), "sx", None, None, None),
            P(("wl", "sy"), "sx", None, None, None, None),
            P(("wl", "sy"), "sx", None, None, None, None),
            P(("wl", "sy"), "sx", None, None, None, None),
            P("wl", None, None),
        ),
        out_specs=(P(("wl", "sy"), "sx", None, None, None, None), P("wl", None, None)),
        check_vma=False,
    )
```

profile of v0, /device:TPU:0, one launch (start us, length us, event | category | flops | bytes accessed | tf_op | source)
XLA Modules:
  0.0 100.0 jit_solution(14972240512666868830)
XLA Ops:
  0.6 1.0 %copy.10 = f32[8,8,4,384]{3,1,2,0:T(8,128)S(1)} copy(f32[8,8,4,384]{3,2,1,0:T(4,128)} %bitcast.18) | data formatting | bytes 786432
  1.7 1.0 %copy.11 = f32[8,8,4,384]{3,1,2,0:T(8,128)S(1)} copy(f32[8,8,4,384]{3,2,1,0:T(4,128)} %bitcast.19) | data formatting | bytes 786432
  2.7 1.2 %copy.9 = f32[16,8,4,384]{3,1,2,0:T(8,128)S(1)} copy(f32[16,8,4,384]{3,2,1,0:T(4,128)} %bitcast.17) | data formatting | bytes 1572864
  3.9 0.0 copy-start
  3.9 9.8 %copy.8 = bf16[192,8,2,1536]{3,1,2,0:T(8,128)(2,1)} copy(bf16[192,8,2,1536]{3,2,1,0:T(2,128)(2,1)} %bitcast.16) | data formatting | bytes 18874368
  13.7 0.0 copy-done
  13.7 84.5 %shard_map.68 = (f32[128,1536]{1,0:T(8,128)S(1)}, f32[2,64,32]{2,1,0:T(8,128)S(1)}) custom-call(bf16[1536,3072]{1,0:T(8,128)(2,1)} %bitcast.15, f32[128,1536]{1,0:T(8,128)S(1)} %bitcast.12, f32[64,1536]{1,0:T(8,128)S(1)} %bitcast.13, f32[64,1536]{1,0:T(8,128)S(1)} %bitcast.14, f32[2,32,32]{2,1,0:T(8,128)S(1)} %copy-done), custom_call_target="tpu_custom_call" | custom-call | tf_op jit(solution)/shard_map/pallas_call | solution.py:331
  98.2 1.1 %reshape.23 = f32[1,1,2,64,4,384]{5,4,3,2,1,0:T(4,128)} reshape(f32[128,1536]{1,0:T(8,128)S(1)} %get-tuple-element.4) | data formatting | bytes 1572864 | tf_op jit(solution)/shard_map/reshape | solution.py:365
  99.3 0.7 copy.7
Async XLA Ops:
  3.9 9.8 %copy-start = (f32[2,32,32]{2,1,0:T(8,128)S(1)}, f32[2,32,32]{2,1,0:T(8,128)}, u32[]{:S(2)}) copy-start(f32[2,32,32]{2,1,0:T(8,128)} %inv_ref.1) | copy-start | bytes 24580
where the time goes:
time: 101 us; the launch traced here: 100 us
  Pallas kernels  84.5 us (84%)
  local copies, waits for them, and re-layouts  14.9 us (15%)
    pallas_call x1, Pallas kernels, per_device(): pl.pallas_call(functools.partial(sweep_kernel, ny, nx, ITERS), out_shape=...  84.5 us
    unnamed x7, local copies, waits for them, and re-layouts  13.7 us

commit v1 on v0

v1 whole, which is shorter than its diff:
```python
import functools

import jax
import jax.numpy as jnp
from jax import lax
from jax.experimental import pallas as pl
from jax.experimental.pallas import tpu as pltpu
from jax.sharding import PartitionSpec as P

ITERS = 6
LANES = 128
F32, BF16 = jnp.float32, jnp.bfloat16
MESH = pl.DeviceIdType.MESH
PRECISE = lax.Precision.HIGHEST
NT = (((1,), (1,)), ((), ()))
PARTS = 4


def dot(a, b):
    return jnp.dot(a, b, preferred_element_type=F32)


def dot_nt(a, b):
    return lax.dot_general(a, b, NT, preferred_element_type=F32)


def split(x):
    hi = x.astype(BF16)
    return hi, (x - hi.astype(F32)).astype(BF16)


def sweep_kernel(
    ny, nx, iters,
    map_hbm, src_ref, rest_ref, lift_ref, inv_ref,
    traces_ref, coef_ref,
    stage, table, abuf, apbuf, recv, cbuf, crecv, lhs, ext_lhs, ext_rhs, eap_rhs,
    wts, part, xs, rowsum, ys, inv_full, prev,
    side_send, side_recv, diag_send, diag_recv,
    x_send, x_recv, y_send, y_recv, map_sem,
):
    _, nsrc, k = src_ref.shape
    side = k // 4
    rows = rest_ref.shape[0]
    nc = rows // 2
    gs = nc
    groups = nsrc // gs
    tiles = k // LANES
    half = gs // 2
    ap_slot = 2 * groups
    y, x = lax.axis_index("sy"), lax.axis_index("sx")
    up, dn, lf, rt = y > 0, y < ny - 1, x > 0, x < nx - 1
    odd = lax.rem(y, 2) == 1
    sides = ((up, -1, 0), (dn, 1, 0), (lf, 0, -1), (rt, 0, 1))
    diags = (
        (up & lf, -1, -1),
        (up & rt, -1, 1),
        (dn & lf, 1, -1),
        (dn & rt, 1, 1),
    )

    def lanes(s):
        return pl.ds(s * side, side)

    kpart = k // PARTS

    def map_copy(h, c):
        at = pl.ds(h * kpart, kpart)
        return pltpu.make_async_copy(map_hbm.at[at, c], stage.at[c, at], map_sem.at[h, c])

    for h in range(PARTS):
        for c in range(tiles):
            map_copy(h, c).start()

    def exchange(slot, src):
        flat, diag, flat_in, diag_in = [], [], [], []
        for d, (cond, dy, dx) in enumerate(sides):
            o = d ^ 1
            dev = {"sy": y + dy, "sx": x + dx}
            flat.append((cond, pltpu.make_async_remote_copy(
                src.at[:, :, lanes(d)], recv.at[slot, :, :, lanes(o)],
                side_send.at[slot, d], side_recv.at[slot, o],
                device_id=dev, device_id_type=MESH)))
            flat_in.append((cond, pltpu.make_async_remote_copy(
                src.at[:, :, lanes(d)], recv.at[slot, :, :, lanes(d)],
                side_send.at[slot, d], side_recv.at[slot, d],
                device_id=dev, device_id_type=MESH)))
        for d, (cond, dy, dx) in enumerate(diags):
            o = 3 - d
            dev = {"sy": y + dy, "sx": x + dx}
            diag.append((cond, pltpu.make_async_remote_copy(
                cbuf.at[slot], crecv.at[slot, o], diag_send.at[slot, d], diag_recv.at[slot, o],
                device_id=dev, device_id_type=MESH)))
            diag_in.append((cond, pltpu.make_async_remote_copy(
                cbuf.at[slot], crecv.at[slot, d], diag_send.at[slot, d], diag_recv.at[slot, d],
                device_id=dev, device_id_type=MESH)))
        return flat, diag, flat_in, diag_in

    def each(items, what):
        for cond, c in items:
            pl.when(cond)(getattr(c, what))

    def send(slot, src):
        flat, diag, _, _ = exchange(slot, src)
        each(diag, "start")
        (_, north), (_, south), west, east = flat
        pl.when(dn & odd)(south.start)
        pl.when(up)(north.start)
        pl.when(dn & jnp.logical_not(odd))(south.start)
        each((west, east), "start")

    def wait_in(slot, src):
        _, _, flat_in, diag_in = exchange(slot, src)
        each(diag_in, "wait_recv")
        each(flat_in, "wait_recv")

    def wait_sent(slot, src):
        flat, diag, _, _ = exchange(slot, src)
        each(flat, "wait_send")
        each(diag, "wait_send")

    def pack_corners(read, dst):
        def column(s, last):
            if last:
                return read((s + 1) * side - LANES)[:, LANES - 1:]
            return read(s * side)[:, 0:1]

        lane = lax.broadcasted_iota(jnp.int32, (rows, LANES), 1)
        block = jnp.zeros((rows, LANES), F32)
        for j, (a, b) in enumerate((
            ((0, 0), (2, 0)), ((0, 1), (3, 0)), ((1, 0), (2, 1)), ((1, 1), (3, 1)),
        )):
            block = jnp.where(lane == j, column(*a) + column(*b), block)
        if rows < LANES:
            block = jnp.concatenate([block, jnp.zeros((LANES - rows, LANES), F32)], axis=0)
        dst[...] = block.T[:8]

    def assemble(slot, write):
        row = lax.broadcasted_iota(jnp.int32, (LANES, LANES), 0)
        block = jnp.zeros((LANES, LANES), F32)
        for j in range(4):
            block = jnp.where(row == j, crecv[slot, j][3 - j:4 - j], block)
        cols = block.T[:rows] * 0.5
        lane = lax.broadcasted_iota(jnp.int32, (rows, LANES), 1)
        ends = ((0, 1), (2, 3), (0, 2), (1, 3))
        for s in range(4):
            for t in range(side // LANES):
                at = s * side + t * LANES
                v = recv[slot, :, :, at:at + LANES].reshape(rows, LANES)
                if t == 0:
                    j = ends[s][0]
                    v = v + jnp.where(lane == 0, cols[:, j:j + 1], 0.0)
                if t == side // LANES - 1:
                    j = ends[s][1]
                    v = v + jnp.where(lane == LANES - 1, cols[:, j:j + 1], 0.0)
                write(at, v)

    def store_lhs(at, v):
        hi, lo = split(v)
        lhs[:rows, at:at + LANES] = hi
        lhs[rows:, at:at + LANES] = lo

    def x_copies(i):
        res = []
        for d in range(1, nx):
            dev = {"sy": y, "sx": lax.rem(x + d, nx)}
            res.append((
                pltpu.make_async_remote_copy(
                    part.at[i], xs.at[i, x], x_send.at[i, d], x_recv.at[i, d],
                    device_id=dev, device_id_type=MESH),
                pltpu.make_async_remote_copy(
                    part.at[i], xs.at[i, lax.rem(x + nx - d, nx)], x_send.at[i, d], x_recv.at[i, d],
                    device_id=dev, device_id_type=MESH)))
        return res

    def y_copies(i):
        res = []
        for d in range(1, ny):
            dev = {"sy": lax.rem(y + d, ny), "sx": x}
            res.append((
                pltpu.make_async_remote_copy(
                    rowsum.at[i], ys.at[i, y], y_send.at[i, d], y_recv.at[i, d],
                    device_id=dev, device_id_type=MESH),
                pltpu.make_async_remote_copy(
                    rowsum.at[i], ys.at[i, lax.rem(y + ny - d, ny)], y_send.at[i, d], y_recv.at[i, d],
                    device_id=dev, device_id_type=MESH)))
        return res

    def restrict_start(i):
        t = dot_nt(lhs[...], wts[...])
        t = t[:rows] + t[rows:]
        t = t + pltpu.roll(t, 2 * nc, 1)
        im = pltpu.roll(t[gs:], nc, 1)
        lane = lax.broadcasted_iota(jnp.int32, (gs, LANES), 1)
        t = t[:gs] + jnp.where((lane < nc) | ((lane >= 2 * nc) & (lane < 3 * nc)), -im, im)
        lane = lax.broadcasted_iota(jnp.int32, (half, LANES), 1)
        t = jnp.where(lane < 2 * nc, t[:half], t[half:])
        part[i] = t
        xs[i, x] = t
        for c, _ in x_copies(i):
            c.start()

    def restrict_turn(i):
        for _, c in x_copies(i):
            c.wait_recv()
        t = xs[i, 0]
        for j in range(1, nx):
            t = t + xs[i, j]
        rowsum[i] = t
        ys[i, y] = t
        for c, _ in y_copies(i):
            c.start()

    def restrict_end(i):
        for _, c in y_copies(i):
            c.wait_recv()
        for c, _ in x_copies(i):
            c.wait_send()
        for c, _ in y_copies(i):
            c.wait_send()
        t = ys[i, 0]
        for j in range(1, ny):
            t = t + ys[i, j]
        lane = lax.broadcasted_iota(jnp.int32, (half, LANES), 1)
        low = lane < 2 * nc
        return jnp.concatenate([jnp.where(low, t, 0.0), jnp.where(low, 0.0, t)], axis=0)

    def coarse(i, g):
        t = jnp.concatenate([restrict_end(i), prev[g]], axis=1)
        c_re = jnp.dot(t, inv_full[0], preferred_element_type=F32, precision=PRECISE)
        c_im = jnp.dot(t, inv_full[1], preferred_element_type=F32, precision=PRECISE)
        lane = lax.broadcasted_iota(jnp.int32, (gs, LANES), 1)
        prev[g] = jnp.where(lane < nc, c_re, jnp.where(lane < 2 * nc, c_im, 0.0))
        c = jnp.concatenate([c_re, c_im], axis=0)
        hi, lo = split(c)
        lane = lax.broadcasted_iota(jnp.int32, (rows, LANES), 1)
        mid = (lane >= nc) & (lane < 2 * nc)
        ext_lhs[g] = jnp.where(mid, lo.astype(F32), hi.astype(F32)).astype(BF16)
        return c_re, c_im

    def feedback(i):
        t = restrict_end(i)
        g_re = jnp.dot(t, inv_full[0, :LANES], preferred_element_type=F32, precision=PRECISE)
        g_im = jnp.dot(t, inv_full[1, :LANES], preferred_element_type=F32, precision=PRECISE)
        inv_full[0, LANES:LANES + nc] = g_re
        inv_full[0, LANES + nc:LANES + 2 * nc] = -g_im
        inv_full[1, LANES:LANES + nc] = g_im
        inv_full[1, LANES + nc:LANES + 2 * nc] = g_re

    def combine(w):
        p, q = w[:, :side], w[:, side:]
        return p[:nc] - q[nc:], q[:nc] + p[nc:]

    def cols(s):
        return pl.ds(s * 2 * side, 2 * side)

    def wide_product(write):
        for s in range(4):
            w = dot(lhs[...], table[:, cols(s)])
            re, im = combine(w[:rows] + w[rows:])
            write(s, re, im)

    def stack_rhs(dst, s, re, im):
        for at, v in ((0, re), (side, im)):
            hi, lo = split(v)
            dst[:, s * 2 * side + at:s * 2 * side + at + side] = jnp.concatenate(
                [hi, hi, lo, jnp.zeros((LANES - 3 * nc, side), BF16)], axis=0)

    for d, (cond, _, _) in enumerate(sides):
        @pl.when(jnp.logical_not(cond))
        def _(d=d):
            for slot in range(2 * groups + 1):
                recv[slot, :, :, lanes(d)] = jnp.zeros((2, gs, side), F32)
    for d, (cond, _, _) in enumerate(diags):
        @pl.when(jnp.logical_not(cond))
        def _(d=d):
            for slot in range(2 * groups + 1):
                crecv[slot, d] = jnp.zeros((8, LANES), F32)

    def source(g):
        return src_ref.at[:, pl.ds(g * gs, gs)]

    for g in range(groups):
        pack_corners(
            lambda at, g=g: src_ref[:, g * gs:(g + 1) * gs, at:at + LANES].reshape(rows, LANES),
            cbuf.at[g])
        send(g, source(g))

    cr, ci = inv_ref[0], inv_ref[1]
    blank = jnp.zeros((nc, LANES - 3 * nc), F32)
    for i, (top, bottom) in enumerate(((cr, -ci), (ci, cr))):
        for j, v in enumerate((top, bottom, top, bottom)):
            inv_full[i, j * nc:(j + 1) * nc] = jnp.concatenate([v, v, v, blank], axis=1)
        inv_full[i, LANES:] = jnp.zeros((LANES, LANES), F32)
    prev[...] = jnp.zeros_like(prev)
    hi, lo = split(rest_ref[...])
    wts[:rows] = hi
    wts[rows:] = lo
    hi, lo = split(lift_ref[...])
    lhs[:rows] = hi
    lhs[rows:] = lo

    r = lax.broadcasted_iota(jnp.int32, (2 * LANES, 2 * LANES), 0)
    c = lax.broadcasted_iota(jnp.int32, (2 * LANES, 2 * LANES), 1)
    pick = jnp.where(r < LANES, 2 * r, 2 * (r - LANES) + 1)
    perm = jnp.where(pick == c, 1.0, 0.0).astype(BF16)
    per_side = side // LANES
    for h in range(PARTS):
        for c in range(tiles):
            map_copy(h, c).wait()

        def separate(t, carry):
            at = pl.multiple_of(h * kpart + t * LANES, LANES)
            for c in range(0, tiles, 2):
                v = jnp.concatenate([
                    stage.at[c + j].reshape(2 * k, LANES)[pl.ds(pl.multiple_of(2 * at, 2 * LANES), 2 * LANES), :]
                    for j in range(2)], axis=1)
                w = dot(perm, v).astype(BF16)
                for j in range(2):
                    s, t = divmod(c + j, per_side)
                    for b in range(2):
                        col = (2 * s + b) * side + t * LANES
                        table[pl.ds(at, LANES), col:col + LANES] = (
                            w[b * LANES:(b + 1) * LANES, j * LANES:(j + 1) * LANES])
            return carry

        lax.fori_loop(0, kpart // LANES, separate, 0)

    def write_ap(s, re, im):
        apbuf[0, :, s * side:(s + 1) * side] = re
        apbuf[1, :, s * side:(s + 1) * side] = im

    wide_product(write_ap)
    pack_corners(lambda at: apbuf[:, :, at:at + LANES].reshape(rows, LANES), cbuf.at[ap_slot])
    send(ap_slot, apbuf)

    def slot_of(n, g):
        return lax.rem(n, 2) * groups + g

    def step(n, g, i, corrected, before):
        wait_in(slot_of(n - 1, g), abuf.at[g])
        assemble(slot_of(n - 1, g), store_lhs)
        restrict_start(i)
        wait_sent(slot_of(n - 1, g), abuf.at[g])
        for s in range(4):
            at = s * side
            w = dot(lhs[:rows], table[:, cols(s)])
            re, im = combine(w)
            abuf[g, 0, :, at:at + side] = re + src_ref[0, g * gs:(g + 1) * gs, at:at + side]
            abuf[g, 1, :, at:at + side] = im + src_ref[1, g * gs:(g + 1) * gs, at:at + side]
        before()
        if corrected:
            for s in range(4):
                at = s * side
                w = dot(ext_lhs[g], ext_rhs[:, cols(s)])
                re, im = combine(w)
                abuf[g, 0, :, at:at + side] += re
                abuf[g, 1, :, at:at + side] += im
        slot = slot_of(n, g)
        pack_corners(lambda at: abuf[g, :, :, at:at + LANES].reshape(rows, LANES), cbuf.at[slot])
        send(slot, abuf.at[g])

    depth = 4
    total = groups * (iters - 1) + 1
    order = [(1, g) for g in range(groups)] + [None]
    order += [(n, g) for n in range(2, iters) for g in range(groups)]

    def small(i):
        if i >= 1:
            restrict_turn((i - 1) % depth)
        if i >= 2:
            finish(i - 2)

    def finish(i):
        if order[i] is None:
            feedback(i % depth)
        else:
            coarse(i % depth, order[i][1])

    for i in range(groups):
        step(1, i, i % depth, False, functools.partial(small, i))

    i = groups
    wait_in(ap_slot, apbuf)
    assemble(ap_slot, store_lhs)
    restrict_start(i % depth)
    for s in range(4):
        at = s * side
        v = (lhs[:rows, at:at + side].astype(F32) + lhs[rows:, at:at + side].astype(F32))
        stack_rhs(eap_rhs, s, v[:nc], v[nc:])
    small(i)
    wide_product(functools.partial(stack_rhs, ext_rhs))

    for g in range(groups):
        i = groups + 1 + g
        step(2, g, i % depth, True, functools.partial(small, i))

    def body(n, carry):
        for g in range(groups):
            i = groups + 1 + (n - 2) * groups + g

            def before():
                restrict_turn(lax.rem(i - 1, depth))
                coarse(lax.rem(i - 2, depth), (g - 2) % groups)

            step(n, g, lax.rem(i, depth), True, before)
        return carry

    lax.fori_loop(3, iters, body, 0)

    restrict_turn((total - 1) % depth)
    for g in range(groups):
        i = total - groups + g
        c_re, c_im = coarse(i % depth, g)
        coef_ref[0, g * gs:(g + 1) * gs] = c_re[:, :nc]
        coef_ref[1, g * gs:(g + 1) * gs] = c_im[:, :nc]
        for s in range(4):
            at = s * side
            w = dot(ext_lhs[g], eap_rhs[:, cols(s)])
            re, im = combine(w)
            traces_ref[0, g * gs:(g + 1) * gs, at:at + side] = re
            traces_ref[1, g * gs:(g + 1) * gs, at:at + side] = im
        slot = ((iters - 1) % 2) * groups + g
        wait_in(slot, abuf.at[g])

        def store_out(at, v):
            traces_ref[:, g * gs:(g + 1) * gs, at:at + LANES] += v.reshape(2, gs, LANES)

        assemble(slot, store_out)
    for g in range(groups):
        wait_sent(((iters - 1) % 2) * groups + g, abuf.at[g])
    wait_sent(ap_slot, apbuf)


def per_device(ny, nx, interface_map, source_trace, restriction, prolongation, coarse_inverse):
    _, _, _, nsrc, _, side = source_trace.shape
    nc = restriction.shape[3]
    k, rows = 4 * side, 2 * nc
    tiles = k // LANES
    groups = nsrc // nc
    slots = 2 * groups + 1
    half = nc // 2
    table = interface_map.reshape(k, 2, tiles, LANES).transpose(0, 2, 1, 3)
    src = source_trace.reshape(2, nsrc, k)
    rest = restriction.reshape(rows, k)
    lift = prolongation.reshape(rows, k)
    dma = pltpu.SemaphoreType.DMA
    vmem = pl.BlockSpec(memory_space=pltpu.VMEM)
    depth = 4
    traces, coef = pl.pallas_call(
        functools.partial(sweep_kernel, ny, nx, ITERS),
        out_shape=(
            jax.ShapeDtypeStruct((2, nsrc, k), F32),
            jax.ShapeDtypeStruct((2, nsrc, nc), F32),
        ),
        in_specs=[pl.BlockSpec(memory_space=pl.ANY)] + [vmem] * 4,
        out_specs=(vmem, vmem),
        scratch_shapes=[
            pltpu.VMEM((tiles, k, 2, LANES), BF16),
            pltpu.VMEM((k, 2 * k), BF16),
            pltpu.VMEM((groups, 2, nc, k), F32),
            pltpu.VMEM((2, nc, k), F32),
            pltpu.VMEM((slots, 2, nc, k), F32),
            pltpu.VMEM((slots, 8, LANES), F32),
            pltpu.VMEM((slots, 4, 8, LANES), F32),
            pltpu.VMEM((2 * rows, k), BF16),
            pltpu.VMEM((groups, rows, LANES), BF16),
            pltpu.VMEM((LANES, 2 * k), BF16),
            pltpu.VMEM((LANES, 2 * k), BF16),
            pltpu.VMEM((2 * rows, k), BF16),
            pltpu.VMEM((depth, half, LANES), F32),
            pltpu.VMEM((depth, nx, half, LANES), F32),
            pltpu.VMEM((depth, half, LANES), F32),
            pltpu.VMEM((depth, ny, half, LANES), F32),
            pltpu.VMEM((2, 2 * LANES, LANES), F32),
            pltpu.VMEM((groups, nc, LANES), F32),
            dma((slots, 4)), dma((slots, 4)), dma((slots, 4)), dma((slots, 4)),
            dma((depth, nx)), dma((depth, nx)), dma((depth, ny)), dma((depth, ny)),
            dma((PARTS, tiles)),
        ],
        compiler_params=pltpu.CompilerParams(
            has_side_effects=True, vmem_limit_bytes=56 * 1024 * 1024
        ),
    )(table, src, rest, lift, coarse_inverse)
    return (
        traces.reshape(source_trace.shape),
        coef,
    )


def solution(mesh):
    return jax.shard_map(
        functools.partial(per_device, mesh.shape["sy"], mesh.shape["sx"]),
        mesh=mesh,
        in_specs=(
            P(("wl", "sy"), "sx", None, None, None),
            P(("wl", "sy"), "sx", None, None, None, None),
            P(("wl", "sy"), "sx", None, None, None, None),
            P(("wl", "sy"), "sx", None, None, None, None),
            P("wl", None, None),
        ),
        out_specs=(P(("wl", "sy"), "sx", None, None, None, None), P("wl", None, None)),
        check_vma=False,
    )
```

time: 101 us -> 91.2 us (0.903)
  local copies, waits for them, and re-layouts: 14.9 us -> 9.68 us
  Pallas kernels: 84.5 us -> 80.6 us
    unnamed x7 -> x3, local copies, waits for them, and re-layouts: 13.7 us -> 5.08 us
    pallas_call x1, Pallas kernels: 84.5 us -> 80.6 us  [per_device(): pl.pallas_call(functools.partial(sweep_kernel, ny, nx, ITERS), out_shape=...]
    reshape x0 -> x1, local copies, waits for them, and re-layouts: none -> 2.33 us  [per_device(): src = source_trace.reshape(2, nsrc, k)]
    reshape x1, local copies, waits for them, and re-layouts: 1.13 us -> 2.27 us  [per_device(): return (traces.reshape(source_trace.shape), coef)]
where the time goes in v1:
time: 91.2 us; the launch traced here: 90.9 us
  Pallas kernels  80.6 us (88%)
  local copies, waits for them, and re-layouts  9.68 us (11%)
    pallas_call x1, Pallas kernels, per_device(): pl.pallas_call(functools.partial(sweep_kernel, ny, nx, ITERS), out_shape=...  80.6 us
    unnamed x3, local copies, waits for them, and re-layouts  5.08 us
    reshape x1, local copies, waits for them, and re-layouts, per_device(): src = source_trace.reshape(2, nsrc, k)  2.33 us
    reshape x1, local copies, waits for them, and re-layouts, per_device(): return (traces.reshape(source_trace.shape), coef)  2.27 us

profile of v1, /device:TPU:0, one launch (start us, length us, event | category | flops | bytes accessed | tf_op | source)
XLA Modules:
  0.0 90.9 jit_solution(5392026173519325586)
XLA Ops:
  0.6 1.8 %copy.8 = f32[8,8,4,384]{3,1,2,0:T(8,128)} copy(f32[8,8,4,384]{3,2,1,0:T(4,128)} %bitcast.12) | data formatting | bytes 786432
  2.4 1.8 %copy.9 = f32[8,8,4,384]{3,1,2,0:T(8,128)} copy(f32[8,8,4,384]{3,2,1,0:T(4,128)} %bitcast.13) | data formatting | bytes 786432
  4.2 2.3 %reshape.20.src_ref = f32[2,64,1536]{2,1,0:T(8,128)} reshape(f32[1,1,2,64,4,384]{5,4,3,2,1,0:T(4,128)} %param.6) | data formatting | bytes 1572864 | tf_op jit(solution)/shard_map/reshape | solution.py:443
  6.5 80.6 %shard_map.68 = (f32[2,64,1536]{2,1,0:T(8,128)}, f32[2,64,32]{2,1,0:T(8,128)}) custom-call(bf16[1536,12,2,128]{3,2,1,0:T(2,128)(2,1)} %bitcast.9, f32[2,64,1536]{2,1,0:T(8,128)} %reshape.20.src_ref, f32[64,1536]{1,0:T(8,128)} %bitcast.10, f32[64,1536]{1,0:T(8,128)} %bitcast.11, f32[2,32,32]{2,1,0:T(8,128)} %inv_ref.1), custom_call_target="tpu_custom_call" | custom-call | tf_op jit(solution)/shard_map/pallas_call | solution.py:449
  87.1 2.3 %reshape.23 = f32[1,1,2,64,4,384]{5,4,3,2,1,0:T(4,128)} reshape(f32[2,64,1536]{2,1,0:T(8,128)} %get-tuple-element.4) | data formatting | bytes 1572864 | tf_op jit(solution)/shard_map/reshape | solution.py:485
  89.4 1.5 %copy.7 = f32[2,64,32]{1,2,0:T(8,128)} copy(f32[2,64,32]{2,1,0:T(8,128)} %get-tuple-element.7) | data formatting | bytes 32768

commit v2 on v1

--- a/solution.py
+++ b/solution.py
@@ -31,17 +31,17 @@
 
 def sweep_kernel(
     ny, nx, iters,
-    map_hbm, src_ref, rest_ref, lift_ref, inv_ref,
+    map_hbm, src_in, rest_in, lift_in, inv_ref,
     traces_ref, coef_ref,
-    stage, table, abuf, apbuf, recv, cbuf, crecv, lhs, ext_lhs, ext_rhs, eap_rhs,
+    src_ref, stage, table, abuf, apbuf, recv, cbuf, crecv, lhs, ext_lhs, ext_rhs, eap_rhs,
     wts, part, xs, rowsum, ys, inv_full, prev,
     side_send, side_recv, diag_send, diag_recv,
     x_send, x_recv, y_send, y_recv, map_sem,
 ):
     _, nsrc, k = src_ref.shape
     side = k // 4
-    rows = rest_ref.shape[0]
-    nc = rows // 2
+    nc = rest_in.shape[1]
+    rows = 2 * nc
     gs = nc
     groups = nsrc // gs
     tiles = k // LANES
@@ -154,10 +154,13 @@
                     v = v + jnp.where(lane == LANES - 1, cols[:, j:j + 1], 0.0)
                 write(at, v)
 
+    def joined(ref, n):
+        return jnp.concatenate([ref[t, :n] for t in range(tiles)], axis=1)
+
     def store_lhs(at, v):
         hi, lo = split(v)
-        lhs[:rows, at:at + LANES] = hi
-        lhs[rows:, at:at + LANES] = lo
+        lhs[at // LANES, :rows] = hi
+        lhs[at // LANES, rows:] = lo
 
     def x_copies(i):
         res = []
@@ -186,7 +189,7 @@
         return res
 
     def restrict_start(i):
-        t = dot_nt(lhs[...], wts[...])
+        t = dot_nt(joined(lhs, 2 * rows), joined(wts, 2 * rows))
         t = t[:rows] + t[rows:]
         t = t + pltpu.roll(t, 2 * nc, 1)
         im = pltpu.roll(t[gs:], nc, 1)
@@ -247,23 +250,24 @@
         inv_full[1, LANES + nc:LANES + 2 * nc] = g_re
 
     def combine(w):
-        p, q = w[:, :side], w[:, side:]
+        p, q = w[:, :LANES], w[:, LANES:]
         return p[:nc] - q[nc:], q[:nc] + p[nc:]
 
-    def cols(s):
-        return pl.ds(s * 2 * side, 2 * side)
+    def pair(ref, c):
+        return jnp.concatenate([ref[2 * c], ref[2 * c + 1]], axis=1)
 
     def wide_product(write):
-        for s in range(4):
-            w = dot(lhs[...], table[:, cols(s)])
+        a = joined(lhs, 2 * rows)
+        for c in range(tiles):
+            w = dot(a, pair(table, c))
             re, im = combine(w[:rows] + w[rows:])
-            write(s, re, im)
-
-    def stack_rhs(dst, s, re, im):
-        for at, v in ((0, re), (side, im)):
+            write(c, re, im)
+
+    def stack_rhs(dst, c, re, im):
+        for b, v in ((0, re), (1, im)):
             hi, lo = split(v)
-            dst[:, s * 2 * side + at:s * 2 * side + at + side] = jnp.concatenate(
-                [hi, hi, lo, jnp.zeros((LANES - 3 * nc, side), BF16)], axis=0)
+            dst[2 * c + b] = jnp.concatenate(
+                [hi, hi, lo, jnp.zeros((LANES - 3 * nc, LANES), BF16)], axis=0)
 
     for d, (cond, _, _) in enumerate(sides):
         @pl.when(jnp.logical_not(cond))
@@ -279,6 +283,15 @@
     def source(g):
         return src_ref.at[:, pl.ds(g * gs, gs)]
 
+    def native(ref, at):
+        n = ref.shape[0] * ref.shape[1]
+        s, t = divmod(at // LANES, side // LANES)
+        return ref.reshape(n * tiles, LANES)[pl.ds(4 * t + s, n, stride=tiles), :]
+
+    for c in range(tiles):
+        at = c * LANES
+        src_ref[:, :, at:at + LANES] = native(src_in, at).reshape(2, nsrc, LANES)
+
     for g in range(groups):
         pack_corners(
             lambda at, g=g: src_ref[:, g * gs:(g + 1) * gs, at:at + LANES].reshape(rows, LANES),
@@ -292,18 +305,17 @@
             inv_full[i, j * nc:(j + 1) * nc] = jnp.concatenate([v, v, v, blank], axis=1)
         inv_full[i, LANES:] = jnp.zeros((LANES, LANES), F32)
     prev[...] = jnp.zeros_like(prev)
-    hi, lo = split(rest_ref[...])
-    wts[:rows] = hi
-    wts[rows:] = lo
-    hi, lo = split(lift_ref[...])
-    lhs[:rows] = hi
-    lhs[rows:] = lo
+    for t in range(tiles):
+        hi, lo = split(native(rest_in, t * LANES))
+        wts[t, :rows] = hi
+        wts[t, rows:] = lo
+    for t in range(tiles):
+        store_lhs(t * LANES, native(lift_in, t * LANES))
 
     r = lax.broadcasted_iota(jnp.int32, (2 * LANES, 2 * LANES), 0)
     c = lax.broadcasted_iota(jnp.int32, (2 * LANES, 2 * LANES), 1)
     pick = jnp.where(r < LANES, 2 * r, 2 * (r - LANES) + 1)
     perm = jnp.where(pick == c, 1.0, 0.0).astype(BF16)
-    per_side = side // LANES
     for h in range(PARTS):
         for c in range(tiles):
             map_copy(h, c).wait()
@@ -316,18 +328,16 @@
                     for j in range(2)], axis=1)
                 w = dot(perm, v).astype(BF16)
                 for j in range(2):
-                    s, t = divmod(c + j, per_side)
                     for b in range(2):
-                        col = (2 * s + b) * side + t * LANES
-                        table[pl.ds(at, LANES), col:col + LANES] = (
+                        table[2 * (c + j) + b, pl.ds(at, LANES)] = (
                             w[b * LANES:(b + 1) * LANES, j * LANES:(j + 1) * LANES])
             return carry
 
         lax.fori_loop(0, kpart // LANES, separate, 0)
 
-    def write_ap(s, re, im):
-        apbuf[0, :, s * side:(s + 1) * side] = re
-        apbuf[1, :, s * side:(s + 1) * side] = im
+    def write_ap(c, re, im):
+        apbuf[0, :, c * LANES:(c + 1) * LANES] = re
+        apbuf[1, :, c * LANES:(c + 1) * LANES] = im
 
     wide_product(write_ap)
     pack_corners(lambda at: apbuf[:, :, at:at + LANES].reshape(rows, LANES), cbuf.at[ap_slot])
@@ -341,20 +351,20 @@
         assemble(slot_of(n - 1, g), store_lhs)
         restrict_start(i)
         wait_sent(slot_of(n - 1, g), abuf.at[g])
-        for s in range(4):
-            at = s * side
-            w = dot(lhs[:rows], table[:, cols(s)])
-            re, im = combine(w)
-            abuf[g, 0, :, at:at + side] = re + src_ref[0, g * gs:(g + 1) * gs, at:at + side]
-            abuf[g, 1, :, at:at + side] = im + src_ref[1, g * gs:(g + 1) * gs, at:at + side]
+        a = joined(lhs, rows)
+        for c in range(tiles):
+            at = c * LANES
+            re, im = combine(dot(a, pair(table, c)))
+            abuf[g, 0, :, at:at + LANES] = re + src_ref[0, g * gs:(g + 1) * gs, at:at + LANES]
+            abuf[g, 1, :, at:at + LANES] = im + src_ref[1, g * gs:(g + 1) * gs, at:at + LANES]
         before()
         if corrected:
-            for s in range(4):
-                at = s * side
-                w = dot(ext_lhs[g], ext_rhs[:, cols(s)])
-                re, im = combine(w)
-                abuf[g, 0, :, at:at + side] += re
-                abuf[g, 1, :, at:at + side] += im
+            e = ext_lhs[g]
+            for c in range(tiles):
+                at = c * LANES
+                re, im = combine(dot(e, pair(ext_rhs, c)))
+                abuf[g, 0, :, at:at + LANES] += re
+                abuf[g, 1, :, at:at + LANES] += im
         slot = slot_of(n, g)
         pack_corners(lambda at: abuf[g, :, :, at:at + LANES].reshape(rows, LANES), cbuf.at[slot])
         send(slot, abuf.at[g])
@@ -383,10 +393,9 @@
     wait_in(ap_slot, apbuf)
     assemble(ap_slot, store_lhs)
     restrict_start(i % depth)
-    for s in range(4):
-        at = s * side
-        v = (lhs[:rows, at:at + side].astype(F32) + lhs[rows:, at:at + side].astype(F32))
-        stack_rhs(eap_rhs, s, v[:nc], v[nc:])
+    for c in range(tiles):
+        v = lhs[c, :rows].astype(F32) + lhs[c, rows:].astype(F32)
+        stack_rhs(eap_rhs, c, v[:nc], v[nc:])
     small(i)
     wide_product(functools.partial(stack_rhs, ext_rhs))
 
@@ -413,12 +422,12 @@
         c_re, c_im = coarse(i % depth, g)
         coef_ref[0, g * gs:(g + 1) * gs] = c_re[:, :nc]
         coef_ref[1, g * gs:(g + 1) * gs] = c_im[:, :nc]
-        for s in range(4):
-            at = s * side
-            w = dot(ext_lhs[g], eap_rhs[:, cols(s)])
-            re, im = combine(w)
-            traces_ref[0, g * gs:(g + 1) * gs, at:at + side] = re
-            traces_ref[1, g * gs:(g + 1) * gs, at:at + side] = im
+        e = ext_lhs[g]
+        for c in range(tiles):
+            at = c * LANES
+            re, im = combine(dot(e, pair(eap_rhs, c)))
+            traces_ref[0, g * gs:(g + 1) * gs, at:at + LANES] = re
+            traces_ref[1, g * gs:(g + 1) * gs, at:at + LANES] = im
         slot = ((iters - 1) % 2) * groups + g
         wait_in(slot, abuf.at[g])
 
@@ -440,9 +449,12 @@
     slots = 2 * groups + 1
     half = nc // 2
     table = interface_map.reshape(k, 2, tiles, LANES).transpose(0, 2, 1, 3)
-    src = source_trace.reshape(2, nsrc, k)
-    rest = restriction.reshape(rows, k)
-    lift = prolongation.reshape(rows, k)
+
+    def by_tiles(v):
+        v = v.reshape(2, v.shape[3], 4, side // LANES, LANES)
+        return v.transpose(0, 1, 3, 2, 4)
+
+    src, rest, lift = by_tiles(source_trace), by_tiles(restriction), by_tiles(prolongation)
     dma = pltpu.SemaphoreType.DMA
     vmem = pl.BlockSpec(memory_space=pltpu.VMEM)
     depth = 4
@@ -455,18 +467,19 @@
         in_specs=[pl.BlockSpec(memory_space=pl.ANY)] + [vmem] * 4,
         out_specs=(vmem, vmem),
         scratch_shapes=[
+            pltpu.VMEM((2, nsrc, k), F32),
             pltpu.VMEM((tiles, k, 2, LANES), BF16),
-            pltpu.VMEM((k, 2 * k), BF16),
+            pltpu.VMEM((2 * tiles, k, LANES), BF16),
             pltpu.VMEM((groups, 2, nc, k), F32),
             pltpu.VMEM((2, nc, k), F32),
             pltpu.VMEM((slots, 2, nc, k), F32),
             pltpu.VMEM((slots, 8, LANES), F32),
             pltpu.VMEM((slots, 4, 8, LANES), F32),
-            pltpu.VMEM((2 * rows, k), BF16),
+            pltpu.VMEM((tiles, 2 * rows, LANES), BF16),
             pltpu.VMEM((groups, rows, LANES), BF16),
-            pltpu.VMEM((LANES, 2 * k), BF16),
-            pltpu.VMEM((LANES, 2 * k), BF16),
-            pltpu.VMEM((2 * rows, k), BF16),
+            pltpu.VMEM((2 * tiles, LANES, LANES), BF16),
+            pltpu.VMEM((2 * tiles, LANES, LANES), BF16),
+            pltpu.VMEM((tiles, 2 * rows, LANES), BF16),
             pltpu.VMEM((depth, half, LANES), F32),
             pltpu.VMEM((depth, nx, half, LANES), F32),
             pltpu.VMEM((depth, half, LANES), F32),

time: 91.2 us -> 85.2 us (0.934)
  local copies, waits for them, and re-layouts: 9.68 us -> 3.79 us
    unnamed x3 -> x1, local copies, waits for them, and re-layouts: 5.08 us -> 1.53 us
    reshape x1 -> x0, local copies, waits for them, and re-layouts: 2.33 us -> none  [per_device(): src = source_trace.reshape(2, nsrc, k)]
where the time goes in v2:
time: 85.2 us; the launch traced here: 84.9 us
  Pallas kernels  80.5 us (94%)
  local copies, waits for them, and re-layouts  3.79 us (4%)
    pallas_call x1, Pallas kernels, per_device(): pl.pallas_call(functools.partial(sweep_kernel, ny, nx, ITERS), out_shape=...  80.5 us
    reshape x1, local copies, waits for them, and re-layouts, per_device(): return (traces.reshape(source_trace.shape), coef)  2.27 us

profile of v2, /device:TPU:0, one launch (start us, length us, event | category | flops | bytes accessed | tf_op | source)
XLA Modules:
  0.0 84.9 jit_solution(6909222986746804964)
XLA Ops:
  0.6 80.5 %shard_map.68 = (f32[2,64,1536]{2,1,0:T(8,128)}, f32[2,64,32]{2,1,0:T(8,128)}) custom-call(bf16[1536,12,2,128]{3,2,1,0:T(2,128)(2,1)} %bitcast.12, f32[2,64,3,4,128]{4,3,2,1,0:T(4,128)} %bitcast.13, f32[2,32,3,4,128]{4,3,2,1,0:T(4,128)} %bitcast.14, f32[2,32,3,4,128]{4,3,2,1,0:T(4,128)} %bitcast.15, f32[2,32,32]{2,1,0:T(8,128)} %inv_ref.1), custom_call_target="tpu_custom_call" | custom-call | tf_op jit(solution)/shard_map/pallas_call | solution.py:461
  81.1 2.3 %reshape.23 = f32[1,1,2,64,4,384]{5,4,3,2,1,0:T(4,128)} reshape(f32[2,64,1536]{2,1,0:T(8,128)} %get-tuple-element.4) | data formatting | bytes 1572864 | tf_op jit(solution)/shard_map/reshape | solution.py:498
  83.4 1.5 %copy.7 = f32[2,64,32]{1,2,0:T(8,128)} copy(f32[2,64,32]{2,1,0:T(8,128)} %get-tuple-element.7) | data formatting | bytes 32768
